TPU v7x, 32 devices: a whole 2x2x4 slice. The times are simulated.
32 devices in a mesh: row: 8 (over z, core), col: 4 (over y, x).
Axes of the slice: x: 2, y: 2, z: 4, core: 2. Of those that a mesh axis runs over, the one named last changes fastest.
Arguments:
- train_weight: bfloat16 [4, 4608, 2048], P(None, 'row', 'col')
- src_map: int32 [16], replicated, may hold values from 0 to 15, as said below
- tgt_map: int32 [16], replicated, may hold values from 0 to 15, as said below
- probe: bfloat16 [4096, 4608], P('row'), may hold values from -6 to 6
Outputs:
- codes: bfloat16 [4, 4608, 2048], P(None, None, 'col')
- peaks: float32 [4, 16], P(None, 'col')
- checked: bfloat16 [4, 4096, 2048], P(None, 'row', 'col')
Inputs may be any that keep to these rules, and one draw needn't show every extreme that they name: src_map is a permutation of 0 to 15. tgt_map is a permutation of 0 to 15. Call column k the slots k * 4 to (k + 1) * 4 - 1 of a map, and let C = 4. There are three different offsets a, b, c in 0 to C - 1, the same for every column, of which one is C / 2 and one is C - 1: the heads of training column k stand in serving columns (k - a) mod C (2 of them), (k - b) mod C (one) and (k - c) mod C (one).
All inputs are finite; a program needn't handle non-finite values. Where the computation divides by a largest or mean magnitude, that divisor is 1e-20 or more.
Results may differ from a plain program's by a relative error of at most 0.0049.
Values may be sent and summed in bfloat16 or wider, within the bound.
A program may use at most 128 MiB of HBM per device.

v0:
```python
import functools

import jax
import jax.numpy as jnp
from jax import lax
from jax.experimental import pallas as pl
from jax.experimental.pallas import tpu as pltpu
from jax.sharding import PartitionSpec as P

HDIM = 128
CORES = 2
TILE = 16
KSTEP = 512
MESH = pl.DeviceIdType.MESH


def pieces_of(rows, most):
    for count in range(most, 0, -1):
        if rows % (TILE * count) == 0:
            return count
    return 1


def piece_list(layers, rows):
    out = []
    for layer in range(layers):
        count = pieces_of(rows, 4 if layer == 0 else (1 if layer == layers - 1 else 2))
        size = rows // count
        for i in range(count):
            out.append((layer, i * size, size))
    return out


def chunk_list(pieces, layers, heads):
    out = []
    for e, (layer, _, _) in enumerate(pieces):
        step = 2 if layer == layers - 1 else heads
        out.extend((e, h0, step) for h0 in range(0, heads, step))
    return out


def kernel(
    pieces, chunks, zs, cols, source_ref, w_ref, probe_ref, codes_ref, checked_ref, peaks_ref,
    full, pbuf, guard,
    csend, crecv, zsend, zrecv, local, probesem, *raws,
):
    layers, heads, width, _ = full.shape
    rows = w_ref.shape[1]
    tokens = pbuf.shape[0]
    me = lax.axis_index("row")
    mycol = lax.axis_index("col")
    z = me // CORES
    core = me % CORES
    partner = z * CORES + (1 - core)
    has_down = z > 0
    has_up = z < zs - 1

    barrier = pltpu.get_barrier_semaphore()
    for o in range(1, cols):
        pl.semaphore_signal(
            barrier, inc=1, device_id={"col": lax.rem(mycol + o, cols)}, device_id_type=MESH
        )
    pl.semaphore_signal(barrier, inc=1, device_id={"row": partner}, device_id_type=MESH)

    @pl.when(has_down)
    def _():
        pl.semaphore_signal(barrier, inc=1, device_id={"row": me - CORES}, device_id_type=MESH)

    @pl.when(has_up)
    def _():
        pl.semaphore_signal(barrier, inc=1, device_id={"row": me + CORES}, device_id_type=MESH)

    pl.semaphore_wait(barrier, cols + has_down.astype(jnp.int32) + has_up.astype(jnp.int32))

    def raw_at(g, owner, head):
        return raws[g].at[owner * heads + head]

    def col_copy(g, owner, target, head):
        layer, r0, size = pieces[g]
        return pltpu.make_async_remote_copy(
            src_ref=w_ref.at[layer, pl.ds(r0, size), pl.ds(head * HDIM, HDIM)],
            dst_ref=raw_at(g, owner, head),
            send_sem=csend.at[g, target, head],
            recv_sem=crecv.at[g, owner, head],
            device_id={"col": target},
            device_id_type=MESH,
        )

    def own_copy(g, head):
        layer, r0, size = pieces[g]
        return pltpu.make_async_copy(
            w_ref.at[layer, pl.ds(r0, size), pl.ds(head * HDIM, HDIM)],
            raw_at(g, mycol, head),
            local.at[g, head],
        )

    for g in range(len(pieces)):
        for head in range(heads):
            for o in range(1, cols):
                col_copy(g, mycol, lax.rem(mycol + o, cols), head).start()
            own_copy(g, head).start()
    probe_copy = pltpu.make_async_copy(probe_ref, pbuf, probesem.at[0])
    probe_copy.start()

    def row_copy(g, zb, cb, way, target):
        piece, h0, hn = chunks[g]
        layer, r0, size = pieces[piece]
        block = zb * CORES + cb
        ref = full.at[layer, pl.ds(h0, hn), pl.ds(pl.multiple_of(block * rows + r0, TILE), size), :]
        return pltpu.make_async_remote_copy(
            src_ref=ref,
            dst_ref=ref,
            send_sem=zsend.at[g, zb, way],
            recv_sem=zrecv.at[g, block],
            device_id={"row": target},
            device_id_type=MESH,
        )

    down, up = me - CORES, me + CORES

    def stage_own(g):
        piece, h0, hn = chunks[g]
        layer, r0, size = pieces[piece]
        for head in range(heads):
            if h0 == 0:
                for o in range(1, cols):
                    col_copy(piece, lax.rem(mycol + o, cols), mycol, head).wait_recv()
                own_copy(piece, head).wait()
        start = pl.multiple_of(me * rows + r0, TILE)

        @pl.loop(h0, h0 + hn)
        def _(t):
            full[layer, t, pl.ds(start, size), :] = raws[piece][source_ref[t]]

        @pl.loop(h0, h0 + hn)
        def _(t):
            block = full[layer, t, pl.ds(start, size), :]
            guard[t] = jnp.max(block.reshape(-1, TILE, HDIM), axis=0)

        @pl.when(has_down)
        def _():
            row_copy(g, z, core, 0, down).start()

        @pl.when(has_up)
        def _():
            row_copy(g, z, core, 1, up).start()

        row_copy(g, z, core, 2, partner).start()

    def stage_forward(g):
        for h in range(1, zs):
            @pl.when(z + h < zs)
            def _():
                row_copy(g, z + h, core, 0, down).wait_recv()

                @pl.when(has_down)
                def _():
                    row_copy(g, z + h, core, 0, down).start()

                row_copy(g, z + h, core, 2, partner).start()

            @pl.when(z - h >= 0)
            def _():
                row_copy(g, z - h, core, 1, up).wait_recv()

                @pl.when(has_up)
                def _():
                    row_copy(g, z - h, core, 1, up).start()

                row_copy(g, z - h, core, 2, partner).start()

    def compute(layer, t0):
        pair = (t0, t0 + 1)

        def most(i, acc):
            at = pl.ds(pl.multiple_of(i * KSTEP, KSTEP), KSTEP)
            return tuple(
                jnp.maximum(
                    acc[t - t0],
                    jnp.max(jnp.abs(full[layer, t, at, :]).reshape(-1, TILE, HDIM), axis=0),
                )
                for t in pair
            )

        zero = jnp.zeros((TILE, HDIM), full.dtype)
        best = lax.fori_loop(0, width // KSTEP, most, (zero,) * 2)
        tops = [
            jnp.max(jnp.max(b.astype(jnp.float32), axis=0, keepdims=True), axis=1, keepdims=True)
            for b in best
        ]
        spread = [jnp.broadcast_to(p, (1, HDIM)) for p in tops]
        inverse = [1.0 / ((p + 1e-06) * 0.25) for p in spread]
        here = lax.broadcasted_iota(jnp.int32, peaks_ref.shape, 0) == layer
        lane = lax.broadcasted_iota(jnp.int32, peaks_ref.shape, 1)
        for t in pair:
            peaks_ref[...] = jnp.where(here & (lane == t), tops[t - t0], peaks_ref[...])

        def step(i, acc):
            at = pl.ds(pl.multiple_of(i * KSTEP, KSTEP), KSTEP)
            both = jnp.concatenate(
                [
                    (
                        (full[layer, t, at, :].astype(jnp.float32) * 0.25) * inverse[t - t0]
                    ).astype(codes_ref.dtype)
                    for t in pair
                ],
                axis=1,
            )
            codes_ref[layer, at, pl.ds(t0 * HDIM, 2 * HDIM)] = both
            return acc + jnp.dot(pbuf[:, at], both, preferred_element_type=jnp.float32)

        acc = lax.fori_loop(0, width // KSTEP, step, jnp.zeros((tokens, 2 * HDIM), jnp.float32))
        scale = jnp.concatenate(spread, axis=1)
        checked_ref[layer, :, pl.ds(t0 * HDIM, 2 * HDIM)] = (acc * scale).astype(
            checked_ref.dtype
        )

    peaks_ref[...] = jnp.zeros_like(peaks_ref)
    total = len(chunks)
    stage_own(0)
    stage_own(1)
    for g in range(total):
        stage_forward(g)
        if g + 2 < total:
            stage_own(g + 2)
        piece, h0, hn = chunks[g]
        layer = pieces[piece][0]
        last = piece + 1 == len(pieces) or pieces[piece + 1][0] != layer
        if last:
            for k, (e, other, _) in enumerate(chunks):
                if pieces[e][0] == layer and other == h0:
                    @pl.loop(0, zs)
                    def _(zb):
                        row_copy(k, zb, 1 - core, 2, partner).wait_recv()
            if layer == 0:
                probe_copy.wait()
            for t0 in range(h0, h0 + hn, 2):
                compute(layer, t0)

    for e in range(len(pieces)):
        for o in range(1, cols):
            for head in range(heads):
                col_copy(e, mycol, lax.rem(mycol + o, cols), head).wait_send()
    for g in range(total):

        @pl.loop(0, zs)
        def _(zb):
            @pl.when(has_down & (zb >= z))
            def _():
                row_copy(g, zb, core, 0, down).wait_send()

            @pl.when(has_up & (zb <= z))
            def _():
                row_copy(g, zb, core, 1, up).wait_send()

            row_copy(g, zb, core, 2, partner).wait_send()


def per_device(train_weight, src_map, tgt_map, probe):
    cols = lax.axis_size("col")
    count = lax.axis_size("row")
    per_col = src_map.shape[0] // cols
    layers, rows, span = train_weight.shape
    tokens, width = probe.shape
    zs = count // CORES
    wanted = lax.dynamic_slice(tgt_map, (lax.axis_index("col") * per_col,), (per_col,))
    source = jnp.argmax(wanted[:, None] == src_map[None, :], axis=1).astype(jnp.int32)
    pieces = piece_list(layers, rows)
    chunks = chunk_list(pieces, layers, per_col)
    total, parts = len(chunks), len(pieces)
    grant = 2 * HDIM * (
        layers * per_col * width + per_col * layers * rows * cols
    ) + 2 * tokens * width + 2**21
    anywhere = pl.BlockSpec(memory_space=pl.ANY)
    smem = pl.BlockSpec(memory_space=pltpu.SMEM)
    dtype = train_weight.dtype
    codes, checked, peaks = pl.pallas_call(
        functools.partial(kernel, pieces, chunks, zs, cols),
        out_shape=(
            pltpu.VMEM((layers, width, span), dtype),
            pltpu.VMEM((layers, tokens, span), dtype),
            jax.ShapeDtypeStruct((layers, per_col), jnp.float32),
        ),
        in_specs=[smem, anywhere, anywhere],
        out_specs=(pl.BlockSpec(memory_space=pltpu.VMEM),) * 3,
        scratch_shapes=[
            pltpu.VMEM((layers, per_col, width, HDIM), dtype),
            pltpu.VMEM((tokens, width), dtype),
            pltpu.VMEM((per_col, TILE, HDIM), dtype),
            pltpu.SemaphoreType.DMA((parts, cols, per_col)),
            pltpu.SemaphoreType.DMA((parts, cols, per_col)),
            pltpu.SemaphoreType.DMA((total, zs, 3)),
            pltpu.SemaphoreType.DMA((total, count)),
            pltpu.SemaphoreType.DMA((parts, per_col)),
            pltpu.SemaphoreType.DMA((1,)),
        ]
        + [pltpu.VMEM((cols * per_col, size, HDIM), dtype) for _, _, size in pieces],
        compiler_params=pltpu.CompilerParams(
            collective_id=0, has_side_effects=True, vmem_limit_bytes=grant
        ),
    )(source, train_weight, probe)
    return codes, peaks, checked


def solution(mesh):
    in_specs = (P(None, "row", "col"), P(), P(), P("row", None))
    out_specs = (P(None, None, "col"), P(None, "col"), P(None, "row", "col"))
    return jax.shard_map(
        per_device, mesh=mesh, in_specs=in_specs, out_specs=out_specs, check_vma=False
    )
```

profile of v0, /device:TPU:0, one launch (start us, length us, event | category | flops | bytes accessed | tf_op | source)
XLA Modules:
  0.0 189.7 jit_solution(5836025221515102666)
XLA Ops:
  0.6 0.7 dynamic_slice.3
  1.4 1.4 iota_reduce_fusion
  2.7 178.2 %shard_map.67 = (bf16[4,4608,512]{2,1,0:T(8,128)(2,1)S(1)}, bf16[4,512,512]{2,1,0:T(8,128)(2,1)S(1)}, f32[4,4]{1,0:T(4,128)S(1)}) custom-call(s32[4]{0:T(128)S(1)} %get-tuple-element.7.source_ref, bf16[4,576,512]{2,1,0:T(8,128)(2,1)} %w_ref.1, bf16[512,4608]{1,0:T(8,128)(2,1)} %probe_ref.1), custom_call_target="tpu_custom_call" | custom-call | tf_op jit(solution)/shard_map/pallas_call | solution.py:277
  180.9 6.9 %copy.10 = bf16[4,4608,512]{2,1,0:T(8,128)(2,1)} copy(bf16[4,4608,512]{2,1,0:T(8,128)(2,1)S(1)} %get-tuple-element.11) | data formatting | bytes 37748736
  187.8 1.3 copy.11
  189.1 0.6 copy.12
where the time goes:
time: 191 us; the launch traced here: 190 us
  Pallas kernels  178 us (93%)
  local copies, waits for them, and re-layouts  9.48 us (5%)
    pallas_call x1, Pallas kernels, per_device(): pl.pallas_call(functools.partial(kernel, pieces, chunks, zs, cols), out_s...  178 us
    unnamed x3, local copies, waits for them, and re-layouts  8.75 us

commit v1 on v0

v1 whole, which is shorter than its diff:
```python
import functools

import jax
import jax.numpy as jnp
from jax import lax
from jax.experimental import pallas as pl
from jax.experimental.pallas import tpu as pltpu
from jax.sharding import PartitionSpec as P

HDIM = 128
CORES = 2
TILE = 16
KSTEP = 512
SLOTS = 2
MESH = pl.DeviceIdType.MESH


def split(rows, shares):
    units, total = rows // TILE, sum(shares)
    cuts = [units * sum(shares[:i]) // total for i in range(len(shares) + 1)]
    return [(a * TILE, (b - a) * TILE) for a, b in zip(cuts, cuts[1:]) if b > a]


def piece_list(layers, rows):
    out = []
    for layer in range(layers):
        shares = (1, 2, 3, 6) if layer == 0 else ((3, 2, 1) if layer == layers - 1 else (1, 1))
        out.extend((layer, r0, size) for r0, size in split(rows, shares))
    return out


def tops_of(read, width, pair):
    def most(i, acc):
        at = pl.ds(pl.multiple_of(i * KSTEP, KSTEP), KSTEP)
        return tuple(
            jnp.maximum(a, jnp.max(jnp.abs(read(t, at)).reshape(-1, TILE, HDIM), axis=0))
            for a, t in zip(acc, pair)
        )

    zero = jnp.zeros((TILE, HDIM), jnp.bfloat16)
    best = lax.fori_loop(0, width // KSTEP, most, (zero,) * len(pair))
    return [
        jnp.max(jnp.max(b.astype(jnp.float32), axis=0, keepdims=True), axis=1, keepdims=True)
        for b in best
    ]


def project(read, write, pbuf, tops, width, pair):
    spread = [jnp.broadcast_to(p, (1, HDIM)) for p in tops]
    inverse = [1.0 / ((p + 1e-06) * 0.25) for p in spread]

    def step(i, acc):
        at = pl.ds(pl.multiple_of(i * KSTEP, KSTEP), KSTEP)
        both = jnp.concatenate(
            [
                ((read(t, at).astype(jnp.float32) * 0.25) * inv).astype(jnp.bfloat16)
                for t, inv in zip(pair, inverse)
            ],
            axis=1,
        )
        write(i, at, both)
        return acc + jnp.dot(pbuf[:, at], both, preferred_element_type=jnp.float32)

    zero = jnp.zeros((pbuf.shape[0], len(pair) * HDIM), jnp.float32)
    acc = lax.fori_loop(0, width // KSTEP, step, zero)
    return acc * jnp.concatenate(spread, axis=1)


def note_tops(peaks_ref, layer, pair, tops):
    here = lax.broadcasted_iota(jnp.int32, peaks_ref.shape, 0) == layer
    lane = lax.broadcasted_iota(jnp.int32, peaks_ref.shape, 1)
    for t, top in zip(pair, tops):
        peaks_ref[...] = jnp.where(here & (lane == t), top, peaks_ref[...])


def gather_kernel(
    pieces, zs, cols, src_map, tgt_map, w_ref, probe_ref,
    checked_ref, last_ref, pbuf, peaks_ref, *refs,
):
    layers, rows, _ = w_ref.shape
    codes_refs, refs = refs[: layers - 1], refs[layers - 1 :]
    (
        full, pack, zown, zpack, zland, guard, table,
        local, probesem, csend, crecv, zsend, zrecv,
        rawsend, rawrecv, rsend, rrecv, psend, precv, *bufs,
    ) = refs
    count = len(pieces)
    own, land = bufs[:count], bufs[count:]
    heads, width, _ = last_ref.shape
    me = lax.axis_index("row")
    mycol = lax.axis_index("col")
    z = me // CORES
    core = me % CORES
    partner = z * CORES + (1 - core)
    down, up = me - CORES, me + CORES
    has_down, has_up = z > 0, z < zs - 1
    low, high = z == 0, z == zs - 1
    is_end = low | high
    near = jnp.where(low, 1, zs - 2)
    first = [g for g in range(count) if pieces[g][0] == 0]

    def layer_ref(layer):
        return last_ref if layer == layers - 1 else full.at[layer]

    def own_copy(g, head):
        layer, r0, size = pieces[g]
        return pltpu.make_async_copy(
            w_ref.at[layer, pl.ds(r0, size), pl.ds(head * HDIM, HDIM)],
            own[g].at[head],
            local.at[g, head],
        )

    def target_of(o):
        return lax.rem(mycol + cols - o, cols)

    barrier = pltpu.get_barrier_semaphore()
    for o in range(1, cols):
        pl.semaphore_signal(barrier, inc=1, device_id={"col": target_of(o)}, device_id_type=MESH)
    pl.semaphore_signal(barrier, inc=1, device_id={"row": partner}, device_id_type=MESH)

    @pl.when(has_down)
    def _():
        pl.semaphore_signal(barrier, inc=1, device_id={"row": down}, device_id_type=MESH)

    @pl.when(has_up)
    def _():
        pl.semaphore_signal(barrier, inc=1, device_id={"row": up}, device_id_type=MESH)

    for g in range(count):
        for head in range(heads):
            own_copy(g, head).start()
    probe_copy = pltpu.make_async_copy(probe_ref, pbuf, probesem.at[0])
    probe_copy.start()
    peaks_ref[...] = jnp.zeros_like(peaks_ref)

    total = cols * heads
    mine = [src_map[mycol * heads + s] for s in range(heads)]
    want = [tgt_map[mycol * heads + t] for t in range(heads)]
    goes = [jnp.int32(0)] * heads
    for p in range(heads, total):
        wanted = tgt_map[p]
        goes = [g + jnp.where(m == wanted, p // heads, 0) for g, m in zip(goes, mine)]
    for o in range(cols):
        to = target_of(o)
        seen, picks = jnp.int32(0), [jnp.int32(0)] * SLOTS
        for s in range(heads):
            hit = goes[s] == to
            picks = [jnp.where(hit & (seen == j), s, q) for j, q in enumerate(picks)]
            seen = seen + jnp.where(hit, 1, 0)
        for j in range(SLOTS):
            table[o * SLOTS + j] = picks[j]
    slot_of = [jnp.int32(0)] * heads
    for c in range(cols):
        seen = jnp.int32(0)
        for s in range(heads):
            held = src_map[c * heads + s]
            for t in range(heads):
                slot_of[t] = jnp.where(want[t] == held, c * SLOTS + seen, slot_of[t])
            hit = want[0] == held
            for t in range(1, heads):
                hit = hit | (want[t] == held)
            seen = jnp.minimum(seen + jnp.where(hit, 1, 0), SLOTS - 1)
    for t in range(heads):
        table[cols * SLOTS + t] = slot_of[t]

    pl.semaphore_wait(barrier, cols + has_down.astype(jnp.int32) + has_up.astype(jnp.int32))

    def raw_copy(g, way, target):
        _, r0, size = pieces[g]
        return pltpu.make_async_remote_copy(
            src_ref=own[g],
            dst_ref=zown.at[:, pl.ds(r0, size), :],
            send_sem=rawsend.at[g, way],
            recv_sem=rawrecv.at[g],
            device_id={"row": target},
            device_id_type=MESH,
        )

    def col_copy(g, o):
        layer, r0, size = pieces[g]
        return pltpu.make_async_remote_copy(
            src_ref=pack.at[layer, o - 1, :, pl.ds(r0, size), :],
            dst_ref=land[g].at[pl.ds(SLOTS * mycol, SLOTS)],
            send_sem=csend.at[g, o],
            recv_sem=crecv.at[g, o],
            device_id={"col": target_of(o)},
            device_id_type=MESH,
        )

    def relay_copy(o):
        return pltpu.make_async_remote_copy(
            src_ref=zpack.at[o - 1],
            dst_ref=zland.at[pl.ds(SLOTS * mycol, SLOTS)],
            send_sem=rsend.at[o],
            recv_sem=rrecv.at[o],
            device_id={"col": target_of(o)},
            device_id_type=MESH,
        )

    def row_copy(g, zb, cb, way, target):
        layer, r0, size = pieces[g]
        block = zb * CORES + cb
        ref = layer_ref(layer).at[:, pl.ds(pl.multiple_of(block * rows + r0, TILE), size), :]
        return pltpu.make_async_remote_copy(
            src_ref=ref,
            dst_ref=ref,
            send_sem=zsend.at[g, zb, way],
            recv_sem=zrecv.at[g, block],
            device_id={"row": target},
            device_id_type=MESH,
        )

    def near_copy(cb):
        start = pl.multiple_of((near * CORES + cb) * rows, TILE)
        ref = full.at[0, :, pl.ds(start, rows), :]
        return pltpu.make_async_remote_copy(
            src_ref=ref,
            dst_ref=ref,
            send_sem=psend.at[0],
            recv_sem=precv.at[0],
            device_id={"row": partner},
            device_id_type=MESH,
        )

    def most_of(block):
        return jnp.max(block.reshape(-1, TILE, HDIM), axis=0)

    def fill(from_ref, out_ref, land_ref):
        for j in range(SLOTS):
            land_ref[SLOTS * mycol + j] = from_ref[table[j]]

        @pl.loop(1, cols)
        def _(o):
            for j in range(SLOTS):
                out_ref[o - 1, j] = from_ref[table[o * SLOTS + j]]

        @pl.loop(1, cols)
        def _(o):
            for j in range(SLOTS):
                guard[j] = most_of(out_ref[o - 1, j])

    def select(land_ref, layer, start, size):
        ref = layer_ref(layer)

        @pl.loop(0, heads)
        def _(t):
            ref[t, pl.ds(start, size), :] = land_ref[table[cols * SLOTS + t]]

        @pl.loop(0, heads)
        def _(t):
            guard[t] = most_of(ref[t, pl.ds(start, size), :])

    def hand_out(g):
        layer, r0, size = pieces[g]
        fill(own[g], pack.at[layer, :, :, pl.ds(r0, size), :], land[g])
        for o in range(1, cols):
            col_copy(g, o).start()

    def wait_own(g):
        for head in range(heads):
            own_copy(g, head).wait()

    def down_goes(g):
        return z > 1 if pieces[g][0] == 0 else has_down

    def up_goes(g):
        return z < zs - 2 if pieces[g][0] == 0 else has_up

    def stage_own(g):
        layer, r0, size = pieces[g]
        for o in range(1, cols):
            col_copy(g, o).wait_recv()
        select(land[g], layer, pl.multiple_of(me * rows + r0, TILE), size)

        @pl.when(down_goes(g))
        def _():
            row_copy(g, z, core, 0, down).start()

        @pl.when(up_goes(g))
        def _():
            row_copy(g, z, core, 1, up).start()

        row_copy(g, z, core, 2, partner).start()

    def stage_forward(g):
        for h in range(1, zs):
            raw = pieces[g][0] == 0 and h == 1

            @pl.when((z + h < zs) & (z > 0) if raw else z + h < zs)
            def _():
                row_copy(g, z + h, core, 0, down).wait_recv()

                @pl.when(has_down)
                def _():
                    row_copy(g, z + h, core, 0, down).start()

                row_copy(g, z + h, core, 2, partner).start()

            @pl.when((z - h >= 0) & (z < zs - 1) if raw else z - h >= 0)
            def _():
                row_copy(g, z - h, core, 1, up).wait_recv()

                @pl.when(has_up)
                def _():
                    row_copy(g, z - h, core, 1, up).start()

                row_copy(g, z - h, core, 2, partner).start()

    def relay_out():
        @pl.when(is_end)
        def _():
            for g in first:
                raw_copy(g, 0, down).wait_recv()
            fill(zown, zpack, zland)
            for o in range(1, cols):
                relay_copy(o).start()

    def relay_in():
        @pl.when(is_end)
        def _():
            for o in range(1, cols):
                relay_copy(o).wait_recv()
            select(zland, 0, pl.multiple_of((near * CORES + core) * rows, TILE), rows)
            near_copy(core).start()

    def wait_partner(layer):
        for g in range(count):
            if pieces[g][0] != layer:
                continue

            @pl.loop(0, zs)
            def _(zb):
                if layer == 0:
                    @pl.when(jnp.logical_not(is_end & (zb == near)))
                    def _():
                        row_copy(g, zb, 1 - core, 2, partner).wait_recv()
                else:
                    row_copy(g, zb, 1 - core, 2, partner).wait_recv()

        if layer == 0:
            @pl.when(is_end)
            def _():
                near_copy(1 - core).wait_recv()

    def compute(layer):
        for t0 in range(0, heads, 2):
            pair = (t0, t0 + 1)

            def read(t, at):
                return full[layer, t, at, :]

            def write(i, at, both):
                codes_refs[layer][at, pl.ds(t0 * HDIM, 2 * HDIM)] = both

            tops = tops_of(read, width, pair)
            note_tops(peaks_ref, layer, pair, tops)
            checked_ref[layer, :, pl.ds(t0 * HDIM, 2 * HDIM)] = project(
                read, write, pbuf, tops, width, pair
            ).astype(checked_ref.dtype)

    for g in first:
        wait_own(g)

        @pl.when(z == 1)
        def _():
            raw_copy(g, 0, down).start()

        @pl.when(z == zs - 2)
        def _():
            raw_copy(g, 1, up).start()

    sent = 0

    def hand_out_layer(layer):
        for g in range(count):
            if pieces[g][0] == layer:
                if layer > 0:
                    wait_own(g)
                hand_out(g)

    hand_out_layer(0)
    hand_out_layer(1)
    stage_own(0)
    stage_own(1)
    for g in range(count):
        stage_forward(g)
        if g + 2 < count:
            stage_own(g + 2)
        if g + 2 == first[-1]:
            relay_out()
            for layer in range(2, layers):
                hand_out_layer(layer)
        layer = pieces[g][0]
        if layer > 0 and pieces[g - 1][0] != layer:
            if layer == 1:
                relay_in()
                probe_copy.wait()
            wait_partner(layer - 1)
            compute(layer - 1)
    wait_partner(layers - 1)

    for g in first:
        @pl.when(z == 1)
        def _():
            raw_copy(g, 0, down).wait_send()

        @pl.when(z == zs - 2)
        def _():
            raw_copy(g, 1, up).wait_send()

    for g in range(count):
        for o in range(1, cols):
            col_copy(g, o).wait_send()

        @pl.loop(0, zs)
        def _(zb):
            goes_down, goes_up = down_goes(g), up_goes(g)

            @pl.when((has_down & (zb > z)) | (goes_down & (zb == z)))
            def _():
                row_copy(g, zb, core, 0, down).wait_send()

            @pl.when((has_up & (zb < z)) | (goes_up & (zb == z)))
            def _():
                row_copy(g, zb, core, 1, up).wait_send()

            if pieces[g][0] == 0:
                @pl.when(jnp.logical_not(is_end & (zb == near)))
                def _():
                    row_copy(g, zb, core, 2, partner).wait_send()
            else:
                row_copy(g, zb, core, 2, partner).wait_send()

    @pl.when(is_end)
    def _():
        for o in range(1, cols):
            relay_copy(o).wait_send()
        near_copy(core).wait_send()


def finish_kernel(
    checked_ref, last_ref, pbuf, peaks_ref, *refs,
):
    done = checked_ref.shape[0]
    codes_refs, refs = refs[:done], refs[done:]
    (
        codes_out, checked_out, peaks_out,
        cbuf, kbuf, tops_ref, codesem, stepsem, checksem, peaksem,
    ) = refs
    heads, width, _ = last_ref.shape
    steps = width // KSTEP
    half = width // 2
    copies = []
    for layer in range(done):
        for i in range(2):
            at = pl.ds(i * half, half)
            copies.append(
                pltpu.make_async_copy(
                    codes_refs[layer].at[at], codes_out.at[layer, at], codesem.at[layer, i]
                )
            )
    copies.append(
        pltpu.make_async_copy(checked_ref, checked_out.at[pl.ds(0, done)], checksem.at[0])
    )
    for copy in copies:
        copy.start()
    tops_ref[...] = peaks_ref[...]

    def step_copy(k, i):
        at = pl.ds(pl.multiple_of(i * KSTEP, KSTEP), KSTEP)
        lanes = pl.ds(k * 2 * HDIM, 2 * HDIM)
        return pltpu.make_async_copy(
            cbuf.at[at, lanes], codes_out.at[done, at, lanes], stepsem.at[k, i]
        )

    def read(t, at):
        return last_ref[t, at, :]

    for t0 in range(0, heads, 2):
        pair = (t0, t0 + 1)

        def write(i, at, both):
            cbuf[at, pl.ds(t0 * HDIM, 2 * HDIM)] = both
            step_copy(t0 // 2, i).start()

        tops = tops_of(read, width, pair)
        note_tops(tops_ref, done, pair, tops)
        kbuf[:, pl.ds(t0 * HDIM, 2 * HDIM)] = project(
            read, write, pbuf, tops, width, pair
        ).astype(kbuf.dtype)
    ends = [
        pltpu.make_async_copy(kbuf, checked_out.at[done], checksem.at[1]),
        pltpu.make_async_copy(tops_ref, peaks_out, peaksem.at[0]),
    ]
    for copy in ends:
        copy.start()
    for copy in copies + ends:
        copy.wait()
    for k in range(heads // 2):
        @pl.loop(0, steps)
        def _(i):
            step_copy(k, i).wait()


def per_device(train_weight, src_map, tgt_map, probe):
    cols = lax.axis_size("col")
    zs = lax.axis_size("row") // CORES
    layers, rows, span = train_weight.shape
    heads = src_map.shape[0] // cols
    tokens, width = probe.shape
    pieces = piece_list(layers, rows)
    count, done = len(pieces), layers - 1
    dtype = train_weight.dtype
    others = cols - 1
    anywhere = pl.BlockSpec(memory_space=pl.ANY)
    vmem = pl.BlockSpec(memory_space=pltpu.VMEM)
    dma = pltpu.SemaphoreType.DMA
    block = 2 * rows * HDIM
    grant = block * (
        done * heads * 2 * zs
        + layers * SLOTS * others
        + heads + SLOTS * others + SLOTS * cols
        + layers * (heads + SLOTS * cols)
    ) + 2**21
    gathered = pl.pallas_call(
        functools.partial(gather_kernel, pieces, zs, cols),
        out_shape=(
            pltpu.VMEM((done, tokens, span), dtype),
            pltpu.VMEM((heads, width, HDIM), dtype),
            pltpu.VMEM((tokens, width), dtype),
            pltpu.VMEM((layers, heads), jnp.float32),
        )
        + (pltpu.VMEM((width, span), dtype),) * done,
        in_specs=[pl.BlockSpec(memory_space=pltpu.SMEM)] * 2 + [anywhere] * 2,
        out_specs=(vmem,) * (4 + done),
        scratch_shapes=[
            pltpu.VMEM((done, heads, width, HDIM), dtype),
            pltpu.VMEM((layers, others, SLOTS, rows, HDIM), dtype),
            pltpu.VMEM((heads, rows, HDIM), dtype),
            pltpu.VMEM((others, SLOTS, rows, HDIM), dtype),
            pltpu.VMEM((cols * SLOTS, rows, HDIM), dtype),
            pltpu.VMEM((heads, TILE, HDIM), dtype),
            pltpu.SMEM((cols * SLOTS + heads,), jnp.int32),
            dma((count, heads)),
            dma((1,)),
            dma((count, cols)),
            dma((count, cols)),
            dma((count, zs, 3)),
            dma((count, zs * CORES)),
            dma((count, 2)),
            dma((count,)),
            dma((cols,)),
            dma((cols,)),
            dma((1,)),
            dma((1,)),
        ]
        + [pltpu.VMEM((heads, size, HDIM), dtype) for _, _, size in pieces]
        + [pltpu.VMEM((cols * SLOTS, size, HDIM), dtype) for _, _, size in pieces],
        compiler_params=pltpu.CompilerParams(
            collective_id=0, has_side_effects=True, vmem_limit_bytes=grant
        ),
    )(src_map, tgt_map, train_weight, probe)
    codes, checked, peaks = pl.pallas_call(
        finish_kernel,
        out_shape=(
            jax.ShapeDtypeStruct((layers, width, span), dtype),
            jax.ShapeDtypeStruct((layers, tokens, span), dtype),
            jax.ShapeDtypeStruct((layers, heads), jnp.float32),
        ),
        in_specs=[vmem] * (4 + done),
        out_specs=(anywhere,) * 3,
        scratch_shapes=[
            pltpu.VMEM((width, span), dtype),
            pltpu.VMEM((tokens, span), dtype),
            pltpu.VMEM((layers, heads), jnp.float32),
            dma((done, 2)),
            dma((heads // 2, width // KSTEP)),
            dma((2,)),
            dma((1,)),
        ],
        compiler_params=pltpu.CompilerParams(
            vmem_limit_bytes=2 * width * span + 2 * tokens * span + 2**22
        ),
    )(*[pltpu.with_memory_space_constraint(x, pltpu.VMEM) for x in gathered])
    return codes, peaks, checked


def solution(mesh):
    in_specs = (P(None, "row", "col"), P(), P(), P("row", None))
    out_specs = (P(None, None, "col"), P(None, "col"), P(None, "row", "col"))
    return jax.shard_map(
        per_device, mesh=mesh, in_specs=in_specs, out_specs=out_specs, check_vma=False
    )
```

time: 191 us -> 178 us (0.932)
  local copies, waits for them, and re-layouts: 9.48 us -> 1.3 us
  Pallas kernels: 178 us -> 176 us
    unnamed x3 -> x4, local copies, waits for them, and re-layouts: 8.75 us -> 1.3 us
    pallas_call x1 -> x2, Pallas kernels: 178 us -> 176 us  [the longest x1 166 us: per_device(): pl.pallas_call(functools.partial(gather_kernel, pieces, zs, cols), out_sh...]
where the time goes in v1:
time: 178 us; the launch traced here: 177 us
  Pallas kernels  176 us (99%)
    pallas_call x1, Pallas kernels, per_device(): pl.pallas_call(functools.partial(gather_kernel, pieces, zs, cols), out_sh...  166 us
    pallas_call x1, Pallas kernels, per_device(): pl.pallas_call(finish_kernel, out_shape=(jax.ShapeDtypeStruct((layers, wi...  9.66 us

profile of v1, /device:TPU:0, one launch (start us, length us, event | category | flops | bytes accessed | tf_op | source)
XLA Modules:
  0.0 177.5 jit_solution(15924016384302027044)
XLA Ops:
  0.6 0.0 copy-start
  0.6 0.6 copy-done
  1.3 0.0 copy-start.1
  1.3 0.7 copy-done.1
  1.9 165.9 %shard_map.67 = (bf16[3,512,512]{2,1,0:T(8,128)(2,1)S(1)}, bf16[4,4608,128]{2,1,0:T(8,128)(2,1)S(1)}, bf16[512,4608]{1,0:T(8,128)(2,1)S(1)}, f32[4,4]{1,0:T(4,12...) custom-call(s32[16]{0:T(128)S(1)} %copy-done, ...), custom_call_target="tpu_custom_call" | custom-call | tf_op jit(solution)/shard_map/pallas_call | solution.py:525
  167.8 9.7 %shard_map.68 = (bf16[4,4608,512]{2,1,0:T(8,128)(2,1)}, bf16[4,512,512]{2,1,0:T(8,128)(2,1)}, f32[4,4]{1,0:T(4,128)}) custom-call(bf16[3,512,512]{2,1,0:T(8,128)(2,1)S(1)} %get-tuple-element.13.checked_ref, bf16[4,4608,128]{2,1,0:T(8,128)(2,1)S(1)} %get-tuple-element.14.last_ref, bf16[512,4608]{1,0:T(8,128)(2,1)S(1)} %get-tuple-element.15.pbuf, ...), custom_call_target="tpu_custom_call" | custom-call | tf_op jit(solution)/shard_map/pallas_call | solution.py:563
Async XLA Ops:
  0.6 0.7 copy-start
  1.3 0.7 copy-start.1

commit v2 on v1

--- a/solution.py
+++ b/solution.py
@@ -10,7 +10,10 @@
 HDIM = 128
 CORES = 2
 TILE = 16
-KSTEP = 512
+PSTEP = 128
+CSTEP = 512
+KSTEP = 4608
+NSTEP = 256
 SLOTS = 2
 MESH = pl.DeviceIdType.MESH
 
@@ -29,59 +32,67 @@
     return out
 
 
-def tops_of(read, width, pair):
+def peaks_of(read, width, heads):
     def most(i, acc):
-        at = pl.ds(pl.multiple_of(i * KSTEP, KSTEP), KSTEP)
+        at = pl.ds(pl.multiple_of(i * PSTEP, PSTEP), PSTEP)
         return tuple(
             jnp.maximum(a, jnp.max(jnp.abs(read(t, at)).reshape(-1, TILE, HDIM), axis=0))
-            for a, t in zip(acc, pair)
+            for t, a in enumerate(acc)
         )
 
     zero = jnp.zeros((TILE, HDIM), jnp.bfloat16)
-    best = lax.fori_loop(0, width // KSTEP, most, (zero,) * len(pair))
+    best = lax.fori_loop(0, width // PSTEP, most, (zero,) * heads)
     return [
         jnp.max(jnp.max(b.astype(jnp.float32), axis=0, keepdims=True), axis=1, keepdims=True)
         for b in best
     ]
 
 
-def project(read, write, pbuf, tops, width, pair):
+def encode(read, write, tops, width):
     spread = [jnp.broadcast_to(p, (1, HDIM)) for p in tops]
     inverse = [1.0 / ((p + 1e-06) * 0.25) for p in spread]
 
-    def step(i, acc):
-        at = pl.ds(pl.multiple_of(i * KSTEP, KSTEP), KSTEP)
-        both = jnp.concatenate(
-            [
-                ((read(t, at).astype(jnp.float32) * 0.25) * inv).astype(jnp.bfloat16)
-                for t, inv in zip(pair, inverse)
-            ],
-            axis=1,
-        )
-        write(i, at, both)
-        return acc + jnp.dot(pbuf[:, at], both, preferred_element_type=jnp.float32)
-
-    zero = jnp.zeros((pbuf.shape[0], len(pair) * HDIM), jnp.float32)
-    acc = lax.fori_loop(0, width // KSTEP, step, zero)
-    return acc * jnp.concatenate(spread, axis=1)
-
-
-def note_tops(peaks_ref, layer, pair, tops):
+    @pl.loop(0, width // CSTEP)
+    def _(i):
+        at = pl.ds(pl.multiple_of(i * CSTEP, CSTEP), CSTEP)
+        for t, inv in enumerate(inverse):
+            scaled = (read(t, at) * 0.25).astype(jnp.float32) * inv
+            write(i, t, at, scaled.astype(jnp.bfloat16))
+
+
+def project(codes_ref, pbuf, out_ref, tops):
+    width, span = codes_ref.shape
+    tokens = pbuf.shape[0]
+    spread = jnp.concatenate([jnp.broadcast_to(p, (1, HDIM)) for p in tops], axis=1)
+    for n0 in range(0, span, NSTEP):
+        lanes = pl.ds(n0, NSTEP)
+
+        def step(i, acc):
+            at = pl.ds(pl.multiple_of(i * KSTEP, KSTEP), KSTEP)
+            return acc + jnp.dot(
+                pbuf[:, at], codes_ref[at, lanes], preferred_element_type=jnp.float32
+            )
+
+        acc = lax.fori_loop(0, width // KSTEP, step, jnp.zeros((tokens, NSTEP), jnp.float32))
+        out_ref[:, lanes] = (acc * spread[:, n0 : n0 + NSTEP]).astype(out_ref.dtype)
+
+
+def note_tops(peaks_ref, layer, tops):
     here = lax.broadcasted_iota(jnp.int32, peaks_ref.shape, 0) == layer
     lane = lax.broadcasted_iota(jnp.int32, peaks_ref.shape, 1)
-    for t, top in zip(pair, tops):
+    for t, top in enumerate(tops):
         peaks_ref[...] = jnp.where(here & (lane == t), top, peaks_ref[...])
 
 
 def gather_kernel(
-    pieces, zs, cols, src_map, tgt_map, w_ref, probe_ref,
+    pieces, zs, cols, src_hbm, tgt_hbm, w_ref, probe_ref,
     checked_ref, last_ref, pbuf, peaks_ref, *refs,
 ):
     layers, rows, _ = w_ref.shape
     codes_refs, refs = refs[: layers - 1], refs[layers - 1 :]
     (
-        full, pack, zown, zpack, zland, guard, table,
-        local, probesem, csend, crecv, zsend, zrecv,
+        full, pack, zown, zpack, zland, guard, table, src_map, tgt_map,
+        mapsem, local, probesem, csend, crecv, zsend, zrecv,
         rawsend, rawrecv, rsend, rrecv, psend, precv, *bufs,
     ) = refs
     count = len(pieces)
@@ -113,6 +124,12 @@
     def target_of(o):
         return lax.rem(mycol + cols - o, cols)
 
+    map_copies = [
+        pltpu.make_async_copy(src_hbm, src_map, mapsem.at[0]),
+        pltpu.make_async_copy(tgt_hbm, tgt_map, mapsem.at[1]),
+    ]
+    for copy in map_copies:
+        copy.start()
     barrier = pltpu.get_barrier_semaphore()
     for o in range(1, cols):
         pl.semaphore_signal(barrier, inc=1, device_id={"col": target_of(o)}, device_id_type=MESH)
@@ -133,6 +150,8 @@
     probe_copy.start()
     peaks_ref[...] = jnp.zeros_like(peaks_ref)
 
+    for copy in map_copies:
+        copy.wait()
     total = cols * heads
     mine = [src_map[mycol * heads + s] for s in range(heads)]
     want = [tgt_map[mycol * heads + t] for t in range(heads)]
@@ -306,22 +325,18 @@
 
                 row_copy(g, z - h, core, 2, partner).start()
 
-    def relay_out():
-        @pl.when(is_end)
-        def _():
-            for g in first:
-                raw_copy(g, 0, down).wait_recv()
-            fill(zown, zpack, zland)
-            for o in range(1, cols):
-                relay_copy(o).start()
-
-    def relay_in():
-        @pl.when(is_end)
-        def _():
-            for o in range(1, cols):
-                relay_copy(o).wait_recv()
-            select(zland, 0, pl.multiple_of((near * CORES + core) * rows, TILE), rows)
-            near_copy(core).start()
+    def relay_out(_):
+        for g in first:
+            raw_copy(g, 0, down).wait_recv()
+        fill(zown, zpack, zland)
+        for o in range(1, cols):
+            relay_copy(o).start()
+
+    def relay_in(_):
+        for o in range(1, cols):
+            relay_copy(o).wait_recv()
+        select(zland, 0, pl.multiple_of((near * CORES + core) * rows, TILE), rows)
+        near_copy(core).start()
 
     def wait_partner(layer):
         for g in range(count):
@@ -343,20 +358,18 @@
                 near_copy(1 - core).wait_recv()
 
     def compute(layer):
-        for t0 in range(0, heads, 2):
-            pair = (t0, t0 + 1)
-
-            def read(t, at):
-                return full[layer, t, at, :]
-
-            def write(i, at, both):
-                codes_refs[layer][at, pl.ds(t0 * HDIM, 2 * HDIM)] = both
-
-            tops = tops_of(read, width, pair)
-            note_tops(peaks_ref, layer, pair, tops)
-            checked_ref[layer, :, pl.ds(t0 * HDIM, 2 * HDIM)] = project(
-                read, write, pbuf, tops, width, pair
-            ).astype(checked_ref.dtype)
+        codes_ref = codes_refs[layer]
+
+        def read(t, at):
+            return full[layer, t, at, :]
+
+        def write(i, t, at, codes):
+            codes_ref[at, pl.ds(t * HDIM, HDIM)] = codes
+
+        tops = peaks_of(read, width, heads)
+        note_tops(peaks_ref, layer, tops)
+        encode(read, write, tops, width)
+        project(codes_ref, pbuf, checked_ref.at[layer], tops)
 
     for g in first:
         wait_own(g)
@@ -368,8 +381,6 @@
         @pl.when(z == zs - 2)
         def _():
             raw_copy(g, 1, up).start()
-
-    sent = 0
 
     def hand_out_layer(layer):
         for g in range(count):
@@ -378,25 +389,53 @@
                     wait_own(g)
                 hand_out(g)
 
+    def run(steps):
+        for stage, g in steps:
+            stage(g)
+
+    def either(ends, mids):
+        @pl.when(is_end)
+        def _():
+            run(ends)
+
+        @pl.when(jnp.logical_not(is_end))
+        def _():
+            run(mids)
+
+    def finish(layer):
+        if layer == 0:
+            probe_copy.wait()
+        wait_partner(layer)
+        compute(layer)
+
+    def of(layer, stage):
+        return [(stage, g) for g in range(count) if pieces[g][0] == layer]
+
     hand_out_layer(0)
     hand_out_layer(1)
-    stage_own(0)
-    stage_own(1)
-    for g in range(count):
-        stage_forward(g)
-        if g + 2 < count:
-            stage_own(g + 2)
-        if g + 2 == first[-1]:
-            relay_out()
-            for layer in range(2, layers):
-                hand_out_layer(layer)
-        layer = pieces[g][0]
-        if layer > 0 and pieces[g - 1][0] != layer:
-            if layer == 1:
-                relay_in()
-                probe_copy.wait()
-            wait_partner(layer - 1)
-            compute(layer - 1)
+    own0, fwd0 = of(0, stage_own), of(0, stage_forward)
+    own1, fwd1 = of(1, stage_own), of(1, stage_forward)
+    lead = own0[:2]
+    for f, o in zip(fwd0, own0[2:] + own1):
+        lead += [f, o]
+    cut = 2 * len(own0) - 2
+    either(own0 + [(relay_out, 0)], lead[:cut])
+    for layer in range(2, layers):
+        hand_out_layer(layer)
+    started = lead[cut:] + fwd0[len(own0) - 2 + len(own1):]
+    rest = [o for o in own1 if o not in lead]
+    either(own1 + fwd0 + [(relay_in, 0)], started + rest)
+    finish(0)
+    later = []
+    for layer in range(2, layers):
+        later += of(layer, stage_own)
+    ahead = len(of(2, stage_own))
+    either(later + fwd1, fwd1[:1] + later[:ahead] + fwd1[1:] + later[ahead:])
+    finish(1)
+    for layer in range(2, layers):
+        run(of(layer, stage_forward))
+        if layer < layers - 1:
+            finish(layer)
     wait_partner(layers - 1)
 
     for g in first:
@@ -448,7 +487,6 @@
         cbuf, kbuf, tops_ref, codesem, stepsem, checksem, peaksem,
     ) = refs
     heads, width, _ = last_ref.shape
-    steps = width // KSTEP
     half = width // 2
     copies = []
     for layer in range(done):
@@ -466,28 +504,22 @@
         copy.start()
     tops_ref[...] = peaks_ref[...]
 
-    def step_copy(k, i):
-        at = pl.ds(pl.multiple_of(i * KSTEP, KSTEP), KSTEP)
-        lanes = pl.ds(k * 2 * HDIM, 2 * HDIM)
-        return pltpu.make_async_copy(
-            cbuf.at[at, lanes], codes_out.at[done, at, lanes], stepsem.at[k, i]
-        )
+    def step_copy(i):
+        at = pl.ds(pl.multiple_of(i * CSTEP, CSTEP), CSTEP)
+        return pltpu.make_async_copy(cbuf.at[at], codes_out.at[done, at], stepsem.at[i])
 
     def read(t, at):
         return last_ref[t, at, :]
 
-    for t0 in range(0, heads, 2):
-        pair = (t0, t0 + 1)
-
-        def write(i, at, both):
-            cbuf[at, pl.ds(t0 * HDIM, 2 * HDIM)] = both
-            step_copy(t0 // 2, i).start()
-
-        tops = tops_of(read, width, pair)
-        note_tops(tops_ref, done, pair, tops)
-        kbuf[:, pl.ds(t0 * HDIM, 2 * HDIM)] = project(
-            read, write, pbuf, tops, width, pair
-        ).astype(kbuf.dtype)
+    def write(i, t, at, codes):
+        cbuf[at, pl.ds(t * HDIM, HDIM)] = codes
+        if t == heads - 1:
+            step_copy(i).start()
+
+    tops = peaks_of(read, width, heads)
+    note_tops(tops_ref, done, tops)
+    encode(read, write, tops, width)
+    project(cbuf, pbuf, kbuf, tops)
     ends = [
         pltpu.make_async_copy(kbuf, checked_out.at[done], checksem.at[1]),
         pltpu.make_async_copy(tops_ref, peaks_out, peaksem.at[0]),
@@ -496,10 +528,40 @@
         copy.start()
     for copy in copies + ends:
         copy.wait()
-    for k in range(heads // 2):
-        @pl.loop(0, steps)
-        def _(i):
-            step_copy(k, i).wait()
+
+    @pl.loop(0, width // CSTEP)
+    def _(i):
+        step_copy(i).wait()
+
+
+def finish(gathered, layers, heads, width, span, tokens, dtype):
+    done = layers - 1
+    anywhere = pl.BlockSpec(memory_space=pl.ANY)
+    vmem = pl.BlockSpec(memory_space=pltpu.VMEM)
+    dma = pltpu.SemaphoreType.DMA
+    codes, checked, peaks = pl.pallas_call(
+        finish_kernel,
+        out_shape=(
+            jax.ShapeDtypeStruct((layers, width, span), dtype),
+            jax.ShapeDtypeStruct((layers, tokens, span), dtype),
+            jax.ShapeDtypeStruct((layers, heads), jnp.float32),
+        ),
+        in_specs=[vmem] * (4 + done),
+        out_specs=(anywhere,) * 3,
+        scratch_shapes=[
+            pltpu.VMEM((width, span), dtype),
+            pltpu.VMEM((tokens, span), dtype),
+            pltpu.VMEM((layers, heads), jnp.float32),
+            dma((done, 2)),
+            dma((width // CSTEP,)),
+            dma((2,)),
+            dma((1,)),
+        ],
+        compiler_params=pltpu.CompilerParams(
+            vmem_limit_bytes=2 * width * span + 2 * tokens * span + 2**22
+        ),
+    )(*[pltpu.with_memory_space_constraint(x, pltpu.VMEM) for x in gathered])
+    return codes, peaks, checked
 
 
 def per_device(train_weight, src_map, tgt_map, probe):
@@ -522,6 +584,7 @@
         + heads + SLOTS * others + SLOTS * cols
         + layers * (heads + SLOTS * cols)
     ) + 2**21
+    maps = [pltpu.with_memory_space_constraint(x, pltpu.HBM) for x in (src_map, tgt_map)]
     gathered = pl.pallas_call(
         functools.partial(gather_kernel, pieces, zs, cols),
         out_shape=(
@@ -531,7 +594,7 @@
             pltpu.VMEM((layers, heads), jnp.float32),
         )
         + (pltpu.VMEM((width, span), dtype),) * done,
-        in_specs=[pl.BlockSpec(memory_space=pltpu.SMEM)] * 2 + [anywhere] * 2,
+        in_specs=[pl.BlockSpec(memory_space=pltpu.HBM)] * 2 + [anywhere] * 2,
         out_specs=(vmem,) * (4 + done),
         scratch_shapes=[
             pltpu.VMEM((done, heads, width, HDIM), dtype),
@@ -541,6 +604,9 @@
             pltpu.VMEM((cols * SLOTS, rows, HDIM), dtype),
             pltpu.VMEM((heads, TILE, HDIM), dtype),
             pltpu.SMEM((cols * SLOTS + heads,), jnp.int32),
+            pltpu.SMEM(src_map.shape, jnp.int32),
+            pltpu.SMEM(tgt_map.shape, jnp.int32),
+            dma((2,)),
             dma((count, heads)),
             dma((1,)),
             dma((count, cols)),
@@ -559,30 +625,8 @@
         compiler_params=pltpu.CompilerParams(
             collective_id=0, has_side_effects=True, vmem_limit_bytes=grant
         ),
-    )(src_map, tgt_map, train_weight, probe)
-    codes, checked, peaks = pl.pallas_call(
-        finish_kernel,
-        out_shape=(
-            jax.ShapeDtypeStruct((layers, width, span), dtype),
-            jax.ShapeDtypeStruct((layers, tokens, span), dtype),
-            jax.ShapeDtypeStruct((layers, heads), jnp.float32),
-        ),
-        in_specs=[vmem] * (4 + done),
-        out_specs=(anywhere,) * 3,
-        scratch_shapes=[
-            pltpu.VMEM((width, span), dtype),
-            pltpu.VMEM((tokens, span), dtype),
-            pltpu.VMEM((layers, heads), jnp.float32),
-            dma((done, 2)),
-            dma((heads // 2, width // KSTEP)),
-            dma((2,)),
-            dma((1,)),
-        ],
-        compiler_params=pltpu.CompilerParams(
-            vmem_limit_bytes=2 * width * span + 2 * tokens * span + 2**22
-        ),
-    )(*[pltpu.with_memory_space_constraint(x, pltpu.VMEM) for x in gathered])
-    return codes, peaks, checked
+    )(*maps, train_weight, probe)
+    return finish(gathered, layers, heads, width, span, tokens, dtype)
 
 
 def solution(mesh):

time: 178 us -> 172 us (0.966)
  Pallas kernels: 176 us -> 171 us
    pallas_call x1, Pallas kernels: 9.66 us -> 7.26 us  [finish(): pl.pallas_call(finish_kernel, out_shape=(jax.ShapeDtypeStruct((layers, wi...]
    pallas_call x1, Pallas kernels: 166 us -> 163 us  [per_device(): pl.pallas_call(functools.partial(gather_kernel, pieces, zs, cols), out_sh...]
where the time goes in v2:
time: 172 us; the launch traced here: 171 us
  Pallas kernels  171 us (99%)
    pallas_call x1, Pallas kernels, per_device(): pl.pallas_call(functools.partial(gather_kernel, pieces, zs, cols), out_sh...  163 us
    pallas_call x1, Pallas kernels, finish(): pl.pallas_call(finish_kernel, out_shape=(jax.ShapeDtypeStruct((layers, wi...  7.26 us

profile of v2, /device:TPU:0, one launch (start us, length us, event | category | flops | bytes accessed | tf_op | source)
XLA Modules:
  0.0 171.4 jit_solution(7197651190711969067)
XLA Ops:
  0.6 163.5 %shard_map.67 = (bf16[3,512,512]{2,1,0:T(8,128)(2,1)S(1)}, bf16[4,4608,128]{2,1,0:T(8,128)(2,1)S(1)}, bf16[512,4608]{1,0:T(8,128)(2,1)S(1)}, f32[4,4]{1,0:T(4,12...) custom-call(s32[16]{0:T(128)} %src_hbm.1, s32[16]{0:T(128)} %tgt_hbm.1, ...), custom_call_target="tpu_custom_call" | custom-call | tf_op jit(solution)/shard_map/pallas_call | solution.py:588
  164.1 7.3 %shard_map.68 = (bf16[4,4608,512]{2,1,0:T(8,128)(2,1)}, bf16[4,512,512]{2,1,0:T(8,128)(2,1)}, f32[4,4]{1,0:T(4,128)}) custom-call(bf16[3,512,512]{2,1,0:T(8,128)(2,1)S(1)} %get-tuple-element.13.checked_ref, bf16[4,4608,128]{2,1,0:T(8,128)(2,1)S(1)} %get-tuple-element.14.last_ref, bf16[512,4608]{1,0:T(8,128)(2,1)S(1)} %get-tuple-element.15.pbuf, ...), custom_call_target="tpu_custom_call" | custom-call | tf_op jit(solution)/shard_map/pallas_call | solution.py:542

commit v3 on v2

v3 whole, which is shorter than its diff:
```python
import functools

import jax
import jax.numpy as jnp
from jax import lax
from jax.experimental import pallas as pl
from jax.experimental.pallas import tpu as pltpu
from jax.sharding import PartitionSpec as P

HDIM = 128
CORES = 2
TILE = 16
PSTEP = 128
CSTEP = 512
KSTEP = 4608
NSTEP = 256
SLOTS = 2
VMEM = 63 * 2**20
MESH = pl.DeviceIdType.MESH


def split(rows, shares):
    units, total = rows // TILE, sum(shares)
    cuts = [units * sum(shares[:i]) // total for i in range(len(shares) + 1)]
    return [(a * TILE, (b - a) * TILE) for a, b in zip(cuts, cuts[1:]) if b > a]


def piece_list(layers, rows):
    out = []
    for layer in range(layers):
        if layer == 0:
            shares = (1, 2, 3, 6)
        elif layer == layers - 1:
            shares = (3, 2, 1)
        else:
            shares = (1, 1) if layer == 1 else (1,)
        out.extend((layer, r0, size) for r0, size in split(rows, shares))
    return out


def raw_parts(pieces, raw):
    parts = {}
    for g in raw:
        layer, _, size = pieces[g]
        parts[layer] = parts.get(layer, 0) + size
    out, place = [], 0
    for layer, size in parts.items():
        out.append((layer, size, place))
        place += size
    return out


def peaks_of(read, width, heads):
    def most(i, acc):
        at = pl.ds(pl.multiple_of(i * PSTEP, PSTEP), PSTEP)
        return tuple(
            jnp.maximum(a, jnp.max(jnp.abs(read(t, at)).reshape(-1, TILE, HDIM), axis=0))
            for t, a in enumerate(acc)
        )

    zero = jnp.zeros((TILE, HDIM), jnp.bfloat16)
    best = lax.fori_loop(0, width // PSTEP, most, (zero,) * heads)
    return [
        jnp.max(jnp.max(b.astype(jnp.float32), axis=0, keepdims=True), axis=1, keepdims=True)
        for b in best
    ]


def encode(read, write, tops, width):
    spread = [jnp.broadcast_to(p, (1, HDIM)) for p in tops]
    inverse = [1.0 / ((p + 1e-06) * 0.25) for p in spread]

    @pl.loop(0, width // CSTEP)
    def _(i):
        at = pl.ds(pl.multiple_of(i * CSTEP, CSTEP), CSTEP)
        for t, inv in enumerate(inverse):
            scaled = (read(t, at) * 0.25).astype(jnp.float32) * inv
            write(i, t, at, scaled.astype(jnp.bfloat16))


def project(codes_ref, pbuf, out_ref, tops):
    width, span = codes_ref.shape
    tokens = pbuf.shape[0]
    spread = jnp.concatenate([jnp.broadcast_to(p, (1, HDIM)) for p in tops], axis=1)
    for n0 in range(0, span, NSTEP):
        lanes = pl.ds(n0, NSTEP)

        def step(i, acc):
            at = pl.ds(pl.multiple_of(i * KSTEP, KSTEP), KSTEP)
            return acc + jnp.dot(
                pbuf[:, at], codes_ref[at, lanes], preferred_element_type=jnp.float32
            )

        acc = lax.fori_loop(0, width // KSTEP, step, jnp.zeros((tokens, NSTEP), jnp.float32))
        out_ref[:, lanes] = (acc * spread[:, n0 : n0 + NSTEP]).astype(out_ref.dtype)


def note_tops(peaks_ref, layer, tops):
    here = lax.broadcasted_iota(jnp.int32, peaks_ref.shape, 0) == layer
    lane = lax.broadcasted_iota(jnp.int32, peaks_ref.shape, 1)
    for t, top in enumerate(tops):
        peaks_ref[...] = jnp.where(here & (lane == t), top, peaks_ref[...])


def gather_kernel(
    pieces, raw, zs, cols, src_hbm, tgt_hbm, w_ref, probe_ref,
    checked_ref, last_ref, pbuf, peaks_ref, *refs,
):
    layers, rows, _ = w_ref.shape
    codes_refs, refs = refs[: layers - 1], refs[layers - 1 :]
    (
        full, pack, zown, zpack, zland, guard, table, src_map, tgt_map,
        mapsem, local, probesem, csend, crecv, zsend, zrecv,
        rawsend, rawrecv, rsend, rrecv, psend, precv, *bufs,
    ) = refs
    count = len(pieces)
    own, land = bufs[:count], bufs[count:]
    heads, width, _ = last_ref.shape
    me = lax.axis_index("row")
    mycol = lax.axis_index("col")
    z = me // CORES
    core = me % CORES
    partner = z * CORES + (1 - core)
    down, up = me - CORES, me + CORES
    has_down, has_up = z > 0, z < zs - 1
    low, high = z == 0, z == zs - 1
    is_end = low | high
    near = jnp.where(low, 1, zs - 2)
    parts = raw_parts(pieces, raw)

    def layer_ref(layer):
        return last_ref if layer == layers - 1 else full.at[layer]

    def own_copy(g, head):
        layer, r0, size = pieces[g]
        return pltpu.make_async_copy(
            w_ref.at[layer, pl.ds(r0, size), pl.ds(head * HDIM, HDIM)],
            own[g].at[head],
            local.at[g, head],
        )

    def target_of(o):
        return lax.rem(mycol + cols - o, cols)

    barrier = pltpu.get_barrier_semaphore()
    for o in range(1, cols):
        pl.semaphore_signal(barrier, inc=1, device_id={"col": target_of(o)}, device_id_type=MESH)
    pl.semaphore_signal(barrier, inc=1, device_id={"row": partner}, device_id_type=MESH)

    @pl.when(has_down)
    def _():
        pl.semaphore_signal(barrier, inc=1, device_id={"row": down}, device_id_type=MESH)

    @pl.when(has_up)
    def _():
        pl.semaphore_signal(barrier, inc=1, device_id={"row": up}, device_id_type=MESH)

    for g in raw:
        for head in range(heads):
            own_copy(g, head).start()
    map_copies = [
        pltpu.make_async_copy(src_hbm, src_map, mapsem.at[0]),
        pltpu.make_async_copy(tgt_hbm, tgt_map, mapsem.at[1]),
    ]
    for copy in map_copies:
        copy.start()
    for g in range(len(raw), count):
        for head in range(heads):
            own_copy(g, head).start()
    probe_copy = pltpu.make_async_copy(probe_ref, pbuf, probesem.at[0])
    probe_copy.start()
    peaks_ref[...] = jnp.zeros_like(peaks_ref)

    pl.semaphore_wait(barrier, cols + has_down.astype(jnp.int32) + has_up.astype(jnp.int32))

    def raw_copy(g, way, target):
        layer, r0, size = pieces[g]
        place = r0 + sum(n for other, n, _ in parts if other < layer)
        return pltpu.make_async_remote_copy(
            src_ref=own[g],
            dst_ref=zown.at[:, pl.ds(place, size), :],
            send_sem=rawsend.at[g, way],
            recv_sem=rawrecv.at[g],
            device_id={"row": target},
            device_id_type=MESH,
        )

    def col_copy(g, o):
        layer, r0, size = pieces[g]
        return pltpu.make_async_remote_copy(
            src_ref=pack.at[layer, o - 1, :, pl.ds(r0, size), :],
            dst_ref=land[g].at[pl.ds(SLOTS * mycol, SLOTS)],
            send_sem=csend.at[g, o],
            recv_sem=crecv.at[g, o],
            device_id={"col": target_of(o)},
            device_id_type=MESH,
        )

    def relay_copy(o):
        return pltpu.make_async_remote_copy(
            src_ref=zpack.at[o - 1],
            dst_ref=zland.at[pl.ds(SLOTS * mycol, SLOTS)],
            send_sem=rsend.at[o],
            recv_sem=rrecv.at[o],
            device_id={"col": target_of(o)},
            device_id_type=MESH,
        )

    def row_copy(g, zb, cb, way, target):
        layer, r0, size = pieces[g]
        block = zb * CORES + cb
        ref = layer_ref(layer).at[:, pl.ds(pl.multiple_of(block * rows + r0, TILE), size), :]
        return pltpu.make_async_remote_copy(
            src_ref=ref,
            dst_ref=ref,
            send_sem=zsend.at[g, zb, way],
            recv_sem=zrecv.at[g, block],
            device_id={"row": target},
            device_id_type=MESH,
        )

    def near_copy(k, cb):
        layer, size, _ = parts[k]
        start = pl.multiple_of((near * CORES + cb) * rows, TILE)
        ref = layer_ref(layer).at[:, pl.ds(start, size), :]
        return pltpu.make_async_remote_copy(
            src_ref=ref,
            dst_ref=ref,
            send_sem=psend.at[k],
            recv_sem=precv.at[k],
            device_id={"row": partner},
            device_id_type=MESH,
        )

    def most_of(block):
        return jnp.max(block.reshape(-1, TILE, HDIM), axis=0)

    def fill(from_ref, out_ref, land_ref):
        for j in range(SLOTS):
            land_ref[SLOTS * mycol + j] = from_ref[table[j]]

        @pl.loop(1, cols)
        def _(o):
            for j in range(SLOTS):
                out_ref[o - 1, j] = from_ref[table[o * SLOTS + j]]

        @pl.loop(1, cols)
        def _(o):
            for j in range(SLOTS):
                guard[j] = most_of(out_ref[o - 1, j])

    def select(land_ref, place, layer, start, size):
        ref = layer_ref(layer)

        @pl.loop(0, heads)
        def _(t):
            ref[t, pl.ds(start, size), :] = land_ref[table[cols * SLOTS + t], pl.ds(place, size), :]

        @pl.loop(0, heads)
        def _(t):
            guard[t] = most_of(ref[t, pl.ds(start, size), :])

    def hand_out(g):
        layer, r0, size = pieces[g]
        fill(own[g], pack.at[layer, :, :, pl.ds(r0, size), :], land[g])
        for o in range(1, cols):
            col_copy(g, o).start()

    def wait_own(g):
        for head in range(heads):
            own_copy(g, head).wait()

    def down_goes(g):
        return z > 1 if g in raw else has_down

    def up_goes(g):
        return z < zs - 2 if g in raw else has_up

    def stage_own(g):
        layer, r0, size = pieces[g]
        for o in range(1, cols):
            col_copy(g, o).wait_recv()
        select(land[g], 0, layer, pl.multiple_of(me * rows + r0, TILE), size)

        @pl.when(down_goes(g))
        def _():
            row_copy(g, z, core, 0, down).start()

        @pl.when(up_goes(g))
        def _():
            row_copy(g, z, core, 1, up).start()

        row_copy(g, z, core, 2, partner).start()

    def stage_forward(g):
        for h in range(1, zs):
            skips = g in raw and h == 1

            @pl.when((z + h < zs) & (z > 0) if skips else z + h < zs)
            def _():
                row_copy(g, z + h, core, 0, down).wait_recv()

                @pl.when(has_down)
                def _():
                    row_copy(g, z + h, core, 0, down).start()

                row_copy(g, z + h, core, 2, partner).start()

            @pl.when((z - h >= 0) & (z < zs - 1) if skips else z - h >= 0)
            def _():
                row_copy(g, z - h, core, 1, up).wait_recv()

                @pl.when(has_up)
                def _():
                    row_copy(g, z - h, core, 1, up).start()

                row_copy(g, z - h, core, 2, partner).start()

    def relay_out(_):
        for g in raw:
            raw_copy(g, 0, down).wait_recv()
        fill(zown, zpack, zland)
        for o in range(1, cols):
            relay_copy(o).start()

    def relay_in(_):
        for o in range(1, cols):
            relay_copy(o).wait_recv()
        start = pl.multiple_of((near * CORES + core) * rows, TILE)
        for k, (layer, size, place) in enumerate(parts):
            select(zland, place, layer, start, size)
            near_copy(k, core).start()

    def wait_partner(g):
        @pl.loop(0, zs)
        def _(zb):
            if g in raw:
                @pl.when(jnp.logical_not(is_end & (zb == near)))
                def _():
                    row_copy(g, zb, 1 - core, 2, partner).wait_recv()
            else:
                row_copy(g, zb, 1 - core, 2, partner).wait_recv()

    def drain(g):
        for o in range(1, cols):
            col_copy(g, o).wait_send()

        @pl.loop(0, zs)
        def _(zb):
            @pl.when((has_down & (zb > z)) | (down_goes(g) & (zb == z)))
            def _():
                row_copy(g, zb, core, 0, down).wait_send()

            @pl.when((has_up & (zb < z)) | (up_goes(g) & (zb == z)))
            def _():
                row_copy(g, zb, core, 1, up).wait_send()

            if g in raw:
                @pl.when(jnp.logical_not(is_end & (zb == near)))
                def _():
                    row_copy(g, zb, core, 2, partner).wait_send()
            else:
                row_copy(g, zb, core, 2, partner).wait_send()

    def drain_raw(_):
        for g in raw:
            @pl.when(z == 1)
            def _():
                raw_copy(g, 0, down).wait_send()

            @pl.when(z == zs - 2)
            def _():
                raw_copy(g, 1, up).wait_send()

    def drain_relay(_):
        for o in range(1, cols):
            relay_copy(o).wait_send()
        for k in range(len(parts)):
            near_copy(k, core).wait_send()

    def compute(layer):
        codes_ref = codes_refs[layer]

        def read(t, at):
            return full[layer, t, at, :]

        def write(i, t, at, codes):
            codes_ref[at, pl.ds(t * HDIM, HDIM)] = codes

        tops = peaks_of(read, width, heads)
        note_tops(peaks_ref, layer, tops)
        encode(read, write, tops, width)
        project(codes_ref, pbuf, checked_ref.at[layer], tops)

    for g in raw:
        wait_own(g)

        @pl.when(z == 1)
        def _():
            raw_copy(g, 0, down).start()

        @pl.when(z == zs - 2)
        def _():
            raw_copy(g, 1, up).start()

    for copy in map_copies:
        copy.wait()
    total = cols * heads
    mine = [src_map[mycol * heads + s] for s in range(heads)]
    want = [tgt_map[mycol * heads + t] for t in range(heads)]
    goes = [jnp.int32(0)] * heads
    for p in range(heads, total):
        wanted = tgt_map[p]
        goes = [g + jnp.where(m == wanted, p // heads, 0) for g, m in zip(goes, mine)]
    for o in range(cols):
        to = target_of(o)
        seen, picks = jnp.int32(0), [jnp.int32(0)] * SLOTS
        for s in range(heads):
            hit = goes[s] == to
            picks = [jnp.where(hit & (seen == j), s, q) for j, q in enumerate(picks)]
            seen = seen + jnp.where(hit, 1, 0)
        for j in range(SLOTS):
            table[o * SLOTS + j] = picks[j]
    slot_of = [jnp.int32(0)] * heads
    for c in range(cols):
        seen = jnp.int32(0)
        for s in range(heads):
            held = src_map[c * heads + s]
            for t in range(heads):
                slot_of[t] = jnp.where(want[t] == held, c * SLOTS + seen, slot_of[t])
            hit = want[0] == held
            for t in range(1, heads):
                hit = hit | (want[t] == held)
            seen = jnp.minimum(seen + jnp.where(hit, 1, 0), SLOTS - 1)
    for t in range(heads):
        table[cols * SLOTS + t] = slot_of[t]

    def hand_out_layer(layer):
        for g in range(count):
            if pieces[g][0] == layer:
                if g not in raw:
                    wait_own(g)
                hand_out(g)

    def run(steps):
        for stage, g in steps:
            stage(g)

    def either(ends, mids):
        @pl.when(is_end)
        def _():
            run(ends)

        @pl.when(jnp.logical_not(is_end))
        def _():
            run(mids)

    def finish(layer):
        if layer == 0:
            probe_copy.wait()
        run(of(layer, wait_partner))
        for k, part in enumerate(parts):
            if part[0] == layer:
                @pl.when(is_end)
                def _():
                    near_copy(k, 1 - core).wait_recv()
        compute(layer)

    def of(layer, stage):
        return [(stage, g) for g in range(count) if pieces[g][0] == layer]

    hand_out_layer(0)
    hand_out_layer(1)
    own0, fwd0 = of(0, stage_own), of(0, stage_forward)
    own1, fwd1 = of(1, stage_own), of(1, stage_forward)
    lead = own0[:2]
    for f, o in zip(fwd0, own0[2:] + own1):
        lead += [f, o]
    cut = 2 * len(own0) - 2
    either(own0 + [(relay_out, 0)], lead[:cut])
    for layer in range(2, layers):
        hand_out_layer(layer)
    started = lead[cut:] + fwd0[len(own0) - 2 + len(own1):]
    started += [o for o in own1 if o not in lead]
    later = []
    for layer in range(2, layers):
        later += of(layer, stage_own)
    ahead = len(of(2, stage_own))
    either(
        own1 + fwd0 + [(relay_in, 0)] + later + fwd1,
        started + fwd1[:1] + later[:ahead] + fwd1[1:] + later[ahead:],
    )
    finish(0)
    finish(1)
    for layer in range(2, layers - 1):
        run(of(layer, stage_forward))
        finish(layer)
    *early, end = of(layers - 1, stage_forward)
    *early_in, end_in = of(layers - 1, wait_partner)
    *drains, end_drain = [(drain, g) for g in range(count)]
    either(
        early + [(drain_raw, 0), (drain_relay, 0)] + drains + early_in + [end],
        early + [end, (drain_raw, 0)] + drains + early_in,
    )
    run([end_in, end_drain])


def finish_kernel(
    checked_ref, last_ref, pbuf, peaks_ref, *refs,
):
    done = checked_ref.shape[0]
    codes_refs, refs = refs[:done], refs[done:]
    (
        codes_out, checked_out, peaks_out,
        cbuf, kbuf, tops_ref, codesem, stepsem, checksem, peaksem,
    ) = refs
    heads, width, _ = last_ref.shape
    half = width // 2
    copies = []
    for layer in range(done):
        for i in range(2):
            at = pl.ds(i * half, half)
            copies.append(
                pltpu.make_async_copy(
                    codes_refs[layer].at[at], codes_out.at[layer, at], codesem.at[layer, i]
                )
            )
    copies.append(
        pltpu.make_async_copy(checked_ref, checked_out.at[pl.ds(0, done)], checksem.at[0])
    )
    for copy in copies:
        copy.start()
    tops_ref[...] = peaks_ref[...]

    def step_copy(i):
        at = pl.ds(pl.multiple_of(i * CSTEP, CSTEP), CSTEP)
        return pltpu.make_async_copy(cbuf.at[at], codes_out.at[done, at], stepsem.at[i])

    def read(t, at):
        return last_ref[t, at, :]

    def write(i, t, at, codes):
        cbuf[at, pl.ds(t * HDIM, HDIM)] = codes
        if t == heads - 1:
            step_copy(i).start()

    tops = peaks_of(read, width, heads)
    note_tops(tops_ref, done, tops)
    encode(read, write, tops, width)
    project(cbuf, pbuf, kbuf, tops)
    ends = [
        pltpu.make_async_copy(kbuf, checked_out.at[done], checksem.at[1]),
        pltpu.make_async_copy(tops_ref, peaks_out, peaksem.at[0]),
    ]
    for copy in ends:
        copy.start()
    for copy in copies + ends:
        copy.wait()

    @pl.loop(0, width // CSTEP)
    def _(i):
        step_copy(i).wait()


def finish(gathered, layers, heads, width, span, tokens, dtype):
    done = layers - 1
    anywhere = pl.BlockSpec(memory_space=pl.ANY)
    vmem = pl.BlockSpec(memory_space=pltpu.VMEM)
    dma = pltpu.SemaphoreType.DMA
    codes, checked, peaks = pl.pallas_call(
        finish_kernel,
        out_shape=(
            jax.ShapeDtypeStruct((layers, width, span), dtype),
            jax.ShapeDtypeStruct((layers, tokens, span), dtype),
            jax.ShapeDtypeStruct((layers, heads), jnp.float32),
        ),
        in_specs=[vmem] * (4 + done),
        out_specs=(anywhere,) * 3,
        scratch_shapes=[
            pltpu.VMEM((width, span), dtype),
            pltpu.VMEM((tokens, span), dtype),
            pltpu.VMEM((layers, heads), jnp.float32),
            dma((done, 2)),
            dma((width // CSTEP,)),
            dma((2,)),
            dma((1,)),
        ],
        compiler_params=pltpu.CompilerParams(
            vmem_limit_bytes=2 * width * span + 2 * tokens * span + 2**22
        ),
    )(*[pltpu.with_memory_space_constraint(x, pltpu.VMEM) for x in gathered])
    return codes, peaks, checked


def per_device(train_weight, src_map, tgt_map, probe):
    cols = lax.axis_size("col")
    zs = lax.axis_size("row") // CORES
    layers, rows, span = train_weight.shape
    heads = src_map.shape[0] // cols
    tokens, width = probe.shape
    pieces = piece_list(layers, rows)
    count, done = len(pieces), layers - 1
    dtype = train_weight.dtype
    others = cols - 1
    anywhere = pl.BlockSpec(memory_space=pl.ANY)
    vmem = pl.BlockSpec(memory_space=pltpu.VMEM)
    dma = pltpu.SemaphoreType.DMA
    lane = 2 * HDIM
    results = lane * (heads * (layers * width + done * tokens)) + lane * tokens * (width // HDIM)

    def scratch(raw):
        extra = sum(size for _, size, _ in raw_parts(pieces, raw))
        return extra, lane * (
            done * heads * width
            + layers * rows * (SLOTS * others + heads + SLOTS * cols)
            + extra * (heads + SLOTS * others + SLOTS * cols)
        ) + 2**21

    raw = [g for g in range(count) if pieces[g][0] == 0]
    if results + scratch(raw + [len(raw)])[1] < VMEM:
        raw = raw + [len(raw)]
    extra, grant = scratch(raw)
    maps = [pltpu.with_memory_space_constraint(x, pltpu.HBM) for x in (src_map, tgt_map)]
    gathered = pl.pallas_call(
        functools.partial(gather_kernel, pieces, raw, zs, cols),
        out_shape=(
            pltpu.VMEM((done, tokens, span), dtype),
            pltpu.VMEM((heads, width, HDIM), dtype),
            pltpu.VMEM((tokens, width), dtype),
            pltpu.VMEM((layers, heads), jnp.float32),
        )
        + (pltpu.VMEM((width, span), dtype),) * done,
        in_specs=[pl.BlockSpec(memory_space=pltpu.HBM)] * 2 + [anywhere] * 2,
        out_specs=(vmem,) * (4 + done),
        scratch_shapes=[
            pltpu.VMEM((done, heads, width, HDIM), dtype),
            pltpu.VMEM((layers, others, SLOTS, rows, HDIM), dtype),
            pltpu.VMEM((heads, extra, HDIM), dtype),
            pltpu.VMEM((others, SLOTS, extra, HDIM), dtype),
            pltpu.VMEM((cols * SLOTS, extra, HDIM), dtype),
            pltpu.VMEM((heads, TILE, HDIM), dtype),
            pltpu.SMEM((cols * SLOTS + heads,), jnp.int32),
            pltpu.SMEM(src_map.shape, jnp.int32),
            pltpu.SMEM(tgt_map.shape, jnp.int32),
            dma((2,)),
            dma((count, heads)),
            dma((1,)),
            dma((count, cols)),
            dma((count, cols)),
            dma((count, zs, 3)),
            dma((count, zs * CORES)),
            dma((count, 2)),
            dma((count,)),
            dma((cols,)),
            dma((cols,)),
            dma((2,)),
            dma((2,)),
        ]
        + [pltpu.VMEM((heads, size, HDIM), dtype) for _, _, size in pieces]
        + [pltpu.VMEM((cols * SLOTS, size, HDIM), dtype) for _, _, size in pieces],
        compiler_params=pltpu.CompilerParams(
            collective_id=0, has_side_effects=True, vmem_limit_bytes=grant
        ),
    )(*maps, train_weight, probe)
    return finish(gathered, layers, heads, width, span, tokens, dtype)


def solution(mesh):
    in_specs = (P(None, "row", "col"), P(), P(), P("row", None))
    out_specs = (P(None, None, "col"), P(None, "col"), P(None, "row", "col"))
    return jax.shard_map(
        per_device, mesh=mesh, in_specs=in_specs, out_specs=out_specs, check_vma=False
    )
```

time: 172 us -> 170 us (0.988)
  Pallas kernels: 171 us -> 169 us
where the time goes in v3:
time: 170 us
  Pallas kernels  169 us (99%)
    pallas_call x1, Pallas kernels, per_device(): pl.pallas_call(functools.partial(gather_kernel, pieces, raw, zs, cols), o...  162 us
    pallas_call x1, Pallas kernels, finish(): pl.pallas_call(finish_kernel, out_shape=(jax.ShapeDtypeStruct((layers, wi...  7.26 us

profile of v3, /device:TPU:0, one launch (start us, length us, event | category | flops | bytes accessed | tf_op | source)
XLA Modules:
  0.0 169.8 jit_solution(12405619734824290443)
XLA Ops:
  0.6 161.9 %shard_map.67 = (bf16[3,512,512]{2,1,0:T(8,128)(2,1)S(1)}, bf16[4,4608,128]{2,1,0:T(8,128)(2,1)S(1)}, bf16[512,4608]{1,0:T(8,128)(2,1)S(1)}, f32[4,4]{1,0:T(4,12...) custom-call(s32[16]{0:T(128)} %src_hbm.1, s32[16]{0:T(128)} %tgt_hbm.1, ...), custom_call_target="tpu_custom_call" | custom-call | tf_op jit(solution)/shard_map/pallas_call | solution.py:624
  162.5 7.3 %shard_map.68 = (bf16[4,4608,512]{2,1,0:T(8,128)(2,1)}, bf16[4,512,512]{2,1,0:T(8,128)(2,1)}, f32[4,4]{1,0:T(4,128)}) custom-call(bf16[3,512,512]{2,1,0:T(8,128)(2,1)S(1)} %get-tuple-element.13.checked_ref, bf16[4,4608,128]{2,1,0:T(8,128)(2,1)S(1)} %get-tuple-element.14.last_ref, bf16[512,4608]{1,0:T(8,128)(2,1)S(1)} %get-tuple-element.15.pbuf, ...), custom_call_target="tpu_custom_call" | custom-call | tf_op jit(solution)/shard_map/pallas_call | solution.py:570

commit v4 on v3

--- a/solution.py
+++ b/solution.py
@@ -31,7 +31,7 @@
         if layer == 0:
             shares = (1, 2, 3, 6)
         elif layer == layers - 1:
-            shares = (3, 2, 1)
+            shares = (2, 1)
         else:
             shares = (1, 1) if layer == 1 else (1,)
         out.extend((layer, r0, size) for r0, size in split(rows, shares))
@@ -168,7 +168,6 @@
         for head in range(heads):
             own_copy(g, head).start()
     probe_copy = pltpu.make_async_copy(probe_ref, pbuf, probesem.at[0])
-    probe_copy.start()
     peaks_ref[...] = jnp.zeros_like(peaks_ref)
 
     pl.semaphore_wait(barrier, cols + has_down.astype(jnp.int32) + has_up.astype(jnp.int32))
@@ -470,14 +469,16 @@
         return [(stage, g) for g in range(count) if pieces[g][0] == layer]
 
     hand_out_layer(0)
-    hand_out_layer(1)
+    probe_copy.start()
     own0, fwd0 = of(0, stage_own), of(0, stage_forward)
     own1, fwd1 = of(1, stage_own), of(1, stage_forward)
     lead = own0[:2]
     for f, o in zip(fwd0, own0[2:] + own1):
         lead += [f, o]
     cut = 2 * len(own0) - 2
-    either(own0 + [(relay_out, 0)], lead[:cut])
+    run(own0[:2])
+    hand_out_layer(1)
+    either(own0[2:] + [(relay_out, 0)], lead[2:cut])
     for layer in range(2, layers):
         hand_out_layer(layer)
     started = lead[cut:] + fwd0[len(own0) - 2 + len(own1):]

time: 170 us -> 170 us (level)
  no operation moved by 1% of the time
where the time goes in v4:
time: 170 us
  Pallas kernels  169 us (99%)
    pallas_call x1, Pallas kernels, per_device(): pl.pallas_call(functools.partial(gather_kernel, pieces, raw, zs, cols), o...  162 us
    pallas_call x1, Pallas kernels, finish(): pl.pallas_call(finish_kernel, out_shape=(jax.ShapeDtypeStruct((layers, wi...  7.26 us

profile of v4, /device:TPU:0, one launch (start us, length us, event | category | flops | bytes accessed | tf_op | source)
XLA Modules:
  0.0 169.6 jit_solution(12572313803064170021)
XLA Ops:
  0.6 161.7 %shard_map.67 = (bf16[3,512,512]{2,1,0:T(8,128)(2,1)S(1)}, bf16[4,4608,128]{2,1,0:T(8,128)(2,1)S(1)}, bf16[512,4608]{1,0:T(8,128)(2,1)S(1)}, f32[4,4]{1,0:T(4,12...) custom-call(s32[16]{0:T(128)} %src_hbm.1, s32[16]{0:T(128)} %tgt_hbm.1, ...), custom_call_target="tpu_custom_call" | custom-call | tf_op jit(solution)/shard_map/pallas_call | solution.py:625
  162.3 7.3 %shard_map.68 = (bf16[4,4608,512]{2,1,0:T(8,128)(2,1)}, bf16[4,512,512]{2,1,0:T(8,128)(2,1)}, f32[4,4]{1,0:T(4,128)}) custom-call(bf16[3,512,512]{2,1,0:T(8,128)(2,1)S(1)} %get-tuple-element.13.checked_ref, bf16[4,4608,128]{2,1,0:T(8,128)(2,1)S(1)} %get-tuple-element.14.last_ref, bf16[512,4608]{1,0:T(8,128)(2,1)S(1)} %get-tuple-element.15.pbuf, ...), custom_call_target="tpu_custom_call" | custom-call | tf_op jit(solution)/shard_map/pallas_call | solution.py:571
